TPU v7x, 256 devices: a whole 4x4x8 slice. The times are simulated.
256 devices in a mesh: band: 32 (over y, z), head: 8 (over x, core).
Axes of the slice: x: 4, y: 4, z: 8, core: 2. Of those that a mesh axis runs over, the one named last changes fastest.
Arguments:
- grid_feat: bfloat16 [524288, 1024], P(('band', 'head')), may hold values from -7 to 7
- mesh_feat: bfloat16 [32768, 1024], P(('band', 'head')), may hold values from -7 to 7
- enc_query: bfloat16 [1024, 1024], replicated, may hold values from -0.1875 to 0.1875
- enc_keyval: bfloat16 [1024, 2048], replicated, may hold values from -0.1875 to 0.1875
- enc_out: bfloat16 [1024, 1024], replicated, may hold values from -0.1875 to 0.1875
- proc_qkv: bfloat16 [3, 1024, 1024], P(None, None, 'head'), may hold values from -0.1875 to 0.1875
- proc_out: bfloat16 [1024, 1024], P('head'), may hold values from -0.1875 to 0.1875
- tile_ids: int32 [512, 8], P(('band', 'head')), may hold values from 0 to 4095, as said below
- key_counts: int32 [512], P(('band', 'head')), may hold values from 128 to 1024, as said below
Outputs:
- mesh_out: bfloat16 [32768, 1024], P(('band', 'head'))
Inputs may be any that keep to these rules, and one draw needn't show every extreme that they name: `tile_ids`: mesh tile m lies on the device that holds mesh rows m * 64; every tile it lists is one of that device's grid tiles (grid rows of the same device) or of the 2 grid tiles just before or just after them. Slots may repeat tiles. `key_counts`: the largest value is reached in every draw.
All inputs are finite; a program needn't handle non-finite values.
Results may differ from a plain program's by a relative error of at most 0.012.
The roundings to bfloat16 on the way count: a program that leaves them out, or rounds other values in their place, can miss the bound.
Values may be sent and summed in bfloat16 or wider, within the bound.
No kernel may reach another device: no remote copies, remote signals or barrier semaphores. Data moves between devices by JAX's collectives and lax.ppermute only.
A program may use at most 128 MiB of HBM per device.

v0:
```python
import math

import jax
import jax.numpy as jnp
from jax import lax
from jax.sharding import PartitionSpec as P

D = 1024
HEADS = 16
HALFW = 512
GT = 128
LIST = 8
MT = 64
HALO_TILES = 2


def padded(shard, sides, width):
    edges = {}
    for axis, dim in sides:
        size, length = (lax.axis_size(axis), shard.shape[dim])
        up = [(i, (i + 1) % size) for i in range(size - 1)]
        last = lax.slice_in_dim(shard, length - width, length, axis=dim)
        first = lax.slice_in_dim(shard, 0, width, axis=dim)
        edges[dim] = (
            lax.ppermute(last, axis, up),
            lax.ppermute(first, axis, [(b, a) for a, b in up]),
        )
    done = []
    for _, dim in sides:
        low, high = edges[dim]
        around = [(width, width) if d in done else (0, 0) for d in range(shard.ndim)]
        shard = jnp.concatenate([jnp.pad(low, around), shard, jnp.pad(high, around)], axis=dim)
        done.append(dim)
    return shard


def from_everyone(shard, axis):
    size = lax.axis_size(axis)
    return lax.all_to_all(
        jnp.broadcast_to(shard[None], (size, *shard.shape)), axis, 0, 0, tiled=True
    )


def laid_out(pieces, dim):
    pieces = jnp.moveaxis(pieces, 0, dim)
    dims = pieces.shape
    return pieces.reshape(*dims[:dim], dims[dim] * dims[dim + 1], *dims[dim + 2 :])


def gathered_copies(shard, axis, dim):
    pieces = from_everyone(shard, axis)
    return laid_out(pieces, dim)


def extended(shard, sides, width):
    for axis, dim in sides:
        size, length = (lax.axis_size(axis), shard.shape[dim])
        up = [(i, (i + 1) % size) for i in range(size - 1)]
        down = [(j, i) for i, j in up]
        last = lax.slice_in_dim(shard, length - width, length, axis=dim)
        first = lax.slice_in_dim(shard, 0, width, axis=dim)
        before = lax.ppermute(last, axis, up)
        after = lax.ppermute(first, axis, down)
        shard = jnp.concatenate([before, shard, after], axis=dim)
    return shard


def masked_softmax(scores, key_mask):
    scores = jnp.where(key_mask, scores, -1e30)
    row_top = jnp.max(scores, axis=-1, keepdims=True)
    weights = jnp.exp(scores - row_top)
    return (weights / jnp.sum(weights, axis=-1, keepdims=True)).astype(jnp.bfloat16)


def local(
    grid_feat, mesh_feat, enc_query, enc_keyval, enc_out, proc_qkv, proc_out, tile_ids, key_counts
):
    grid_count, model_width = grid_feat.shape
    mesh_count = mesh_feat.shape[0]
    tiles_dev = grid_count // GT
    head_size = D // HEADS
    score_scale = head_size ** (-0.5)
    device = lax.axis_index(("band", "head"))
    flat_rows = grid_feat.reshape(tiles_dev, GT * model_width)
    bordered = padded(flat_rows, ((("band", "head"), 0),), HALO_TILES)
    grid_kv = jnp.dot(
        bordered.reshape(-1, model_width), enc_keyval, preferred_element_type=jnp.float32
    ).astype(jnp.bfloat16)
    grid_tiles = grid_kv.reshape(-1, GT, 2 * model_width)
    queries = jnp.dot(mesh_feat, enc_query, preferred_element_type=jnp.float32).astype(jnp.bfloat16)
    local_lists = tile_ids - (device * tiles_dev - HALO_TILES)
    positions = jnp.arange(LIST * GT, dtype=jnp.int32)

    def one_tile(packed):
        query_tile, tile_list, valid = packed
        gathered = grid_tiles[tile_list].reshape(LIST * GT, 2 * model_width)
        key_rows = gathered[:, :model_width].reshape(LIST * GT, HEADS, head_size)
        value_rows = gathered[:, model_width:].reshape(LIST * GT, HEADS, head_size)
        query_heads = query_tile.reshape(MT, HEADS, head_size)
        scores = (
            jnp.einsum("qhd,khd->hqk", query_heads, key_rows, preferred_element_type=jnp.float32)
            * score_scale
        )
        weights = masked_softmax(scores, (positions < valid)[None, None, :])
        attended = jnp.einsum(
            "hqk,khd->qhd", weights, value_rows, preferred_element_type=jnp.float32
        )
        return attended.reshape(MT, model_width).astype(jnp.bfloat16)

    enc_attn = lax.map(
        one_tile, (queries.reshape(mesh_count // MT, MT, model_width), local_lists, key_counts)
    )
    enc_attn = enc_attn.reshape(mesh_count, model_width)
    mesh_state = (
        mesh_feat.astype(jnp.float32)
        + jnp.dot(enc_attn, enc_out, preferred_element_type=jnp.float32)
    ).astype(jnp.bfloat16)
    head_cols = proc_qkv.shape[2]
    piece = gathered_copies(mesh_state, "head", 0)
    product = jnp.einsum("rd,tdc->rtc", piece, proc_qkv, preferred_element_type=jnp.float32)
    projected = product.astype(jnp.bfloat16).reshape(piece.shape[0], 3 * head_cols)
    group_rows = projected.shape[0]
    bordered_kv = extended(projected[:, head_cols:], (("band", 0),), HALFW)
    local_heads = head_cols // head_size
    block_rows = math.gcd(group_rows, 512)
    band_start = lax.axis_index("band") * group_rows
    mesh_total = group_rows * lax.axis_size("band")

    def one_block(block_index):
        first = block_index * block_rows
        span = block_rows + 2 * HALFW
        query_heads = lax.dynamic_slice_in_dim(projected, first, block_rows, 0)[
            :, :head_cols
        ].reshape(block_rows, local_heads, head_size)
        window_rows = lax.dynamic_slice_in_dim(bordered_kv, first, span, 0)
        key_rows = window_rows[:, :head_cols].reshape(span, local_heads, head_size)
        value_rows = window_rows[:, head_cols:].reshape(span, local_heads, head_size)
        query_pos = band_start + first + jnp.arange(block_rows, dtype=jnp.int32)
        key_pos = band_start + first - HALFW + jnp.arange(span, dtype=jnp.int32)
        near = (jnp.abs(query_pos[:, None] - key_pos[None, :]) < HALFW) & (
            (key_pos >= 0) & (key_pos < mesh_total)
        )[None, :]
        scores = (
            jnp.einsum("qhd,khd->hqk", query_heads, key_rows, preferred_element_type=jnp.float32)
            * score_scale
        )
        weights = masked_softmax(scores, near[None, :, :])
        attended = jnp.einsum(
            "hqk,khd->qhd", weights, value_rows, preferred_element_type=jnp.float32
        )
        return attended.reshape(block_rows, head_cols).astype(jnp.bfloat16)

    proc_attn = lax.map(one_block, jnp.arange(group_rows // block_rows, dtype=jnp.int32)).reshape(
        group_rows, head_cols
    )
    own_rows = lax.all_to_all(proc_attn, "head", split_axis=0, concat_axis=1, tiled=True)
    out_weights = gathered_copies(proc_out, "head", 0)
    head_total = jnp.dot(own_rows, out_weights, preferred_element_type=jnp.float32)
    return (mesh_state.astype(jnp.float32) + head_total).astype(jnp.bfloat16)


def solution(mesh):
    return jax.shard_map(
        local,
        mesh=mesh,
        in_specs=(
            P(("band", "head"), None),
            P(("band", "head"), None),
            P(),
            P(),
            P(),
            P(None, None, "head"),
            P("head", None),
            P(("band", "head"), None),
            P(("band", "head")),
        ),
        out_specs=P(("band", "head"), None),
        check_vma=False,
    )
```

profile of v0, /device:TPU:24, one launch (start us, length us, event | category | flops | bytes accessed | tf_op | source)
XLA Modules:
  0.0 201.1 jit_solution(4631200154052182882)
XLA Ops:
  5.7 9.6 %collective-permute-start.1 = (bf16[2,131072]{1,0:T(2,128)(2,1)}, bf16[2,131072]{1,0:T(2,128)(2,1)}, u32[]{:S(2)}, u32[]{:S(2)}) collective-permute-start(bf16[2,131072]{1,0:T(2,128)(2,1)} %slice.50), channel_id=1, source_target_pairs={{1,0},{2,1},{3,2},{4,3},{5,4},{6,5},{7,6},{8,7},{9,8},{10,9},{11,1... | collective-permute-start | bytes 1572872 | tf_op jit(solution)/shard_map/ppermute | solution.py:26
  15.3 4.9 %reshape.186 = bf16[16,131072]{1,0:T(8,128)(2,1)} reshape(bf16[2048,1024]{1,0:T(8,128)(2,1)} %param.13) | data formatting | bytes 8388608 | tf_op jit(solution)/shard_map/reshape | solution.py:84
  22.2 7.2 %pad_maximum_fusion = bf16[20,131072]{1,0:T(8,128)(2,1)} fusion(bf16[2,131072]{1,0:T(2,128)(2,1)} %collective-permute-done.1, bf16[16,131072]{1,0:T(8,128)(2,1)} %reshape.186, bf16[2,131072]{1,0:T(2,128)(2,1)S(1)} %collective-permute-done), kind=kLoop, calls=%fused_computation.49 | loop fusion | flops 15728640 | bytes 10485760 | tf_op jit(solution)/shard_map/concatenate | solution.py:32
  29.5 8.2 %reshape.187 = bf16[2560,1024]{1,0:T(8,128)(2,1)} reshape(bf16[20,131072]{1,0:T(8,128)(2,1)} %pad_maximum_fusion) | data formatting | bytes 10485760 | tf_op jit(solution)/shard_map/reshape | solution.py:87
  37.7 16.6 %convolution_convert_fusion = bf16[2560,2048]{1,0:T(8,128)(2,1)} fusion(bf16[2560,1024]{1,0:T(8,128)(2,1)} %reshape.187, bf16[1024,2048]{1,0:T(8,128)(2,1)} %param.16), kind=kOutput, calls=%fused_computation.48 | convolution fusion | flops 10742661120 | bytes 19922944 | tf_op jit(solution)/shard_map/dot_general | solution.py:86
  54.3 52.5 %while.24 = (s32[]{:T(128)}, bf16[2,64,1024]{2,1,0:T(8,128)(2,1)S(1)}, s32[2,8]{1,0:T(2,128)S(1)}, bf16[20,128,2048]{2,1,0:T(8,128)(2,1)}, s32[2]{0:T(128)S(1)}, /*index=5*/bf16[2,64,1024]{2,1,0:T(8,128)(2,1)S(1)}, s32[]{:T(128)}) while((s32[]{:T(128)}, bf16[2,64,1024]{2,1,0:T(8,128)(2,1)S(1)}, s32[2,8]{1,0:T(2,128)S(1)}, ...), condition=%wide.region_3.4_spmd.clone, body=%wide.region_0.3_spmd.clone.sunk | while | flops 276892704 | bytes 55851268 | solution.py:110
  54.3 6.9 %gather_fusion = bf16[8,128,2048]{2,1,0:T(8,128)(2,1)} fusion(bf16[20,128,2048]{2,1,0:T(8,128)(2,1)} %get-tuple-element.272, s32[1024]{0:T(1024)S(1)} %pad_clamp_fusion.2), kind=kCustom, calls=%fused_computation.clone.clone.1 | custom fusion | bytes 8388640 | tf_op jit(solution)/shard_map/while/body/eval_jaxpr/gather | solution.py:96
  61.2 4.7 %fusion.86 = (bf16[1024,1024]{1,0:T(8,128)(2,1)}, bf16[1024,1024]{1,0:T(8,128)(2,1)}) fusion(bf16[1024,2048]{1,0:T(8,128)(2,1)} %bitcast.95), kind=kLoop, calls=%fused_computation.60.clone.1 | loop fusion | bytes 8388608 | tf_op jit(solution)/shard_map/while/body/eval_jaxpr/slice | solution.py:97
  65.8 2.9 %copy.36 = bf16[1024,1024]{0,1:T(8,128)(2,1)S(1)} copy(bf16[1024,1024]{1,0:T(8,128)(2,1)} %get-tuple-element.252) | data formatting | bytes 4194304 | tf_op jit(solution)/shard_map/while
  70.8 3.3 %fusion.88 = (f32[16,64]{1,0:T(8,128)S(1)}, f32[16,64,1024]{2,1,0:T(8,128)}) fusion(f32[16,64,1024]{2,1,0:T(8,128)S(1)} %fusion.87, pred[1024]{0:T(1024)(128)(4,1)S(1)} %iota_compare_fusion.2), kind=kOutput, calls=%fused_computation.61.clone.1 | output fusion | flops 6292479 | bytes 8393728 | tf_op jit(solution)/shard_map/while/body/eval_jaxpr/sub | solution.py:71
  76.7 3.6 %fusion.89 = bf16[16,64,64]{2,1,0:T(8,128)(2,1)S(1)} fusion(bf16[1024,16,64]{0,2,1:T(8,128)(2,1)} %bitcast.97, f32[16,64,1024]{2,1,0:T(8,128)} %get-tuple-element.253, f32[16,64]{1,0:T(8,128)S(1)} %get-tuple-element.254), kind=kOutput, calls=%fused_computation.35.clone.1 | convolution fusion | flops 136380416 | bytes 6426624 | tf_op jit(solution)/shard_map/while/body/eval_jaxpr/hqk,khd->qhd/dot_general | solution.py:105
  80.5 6.9 %gather_fusion = bf16[8,128,2048]{2,1,0:T(8,128)(2,1)} fusion(bf16[20,128,2048]{2,1,0:T(8,128)(2,1)} %get-tuple-element.272, s32[1024]{0:T(1024)S(1)} %pad_clamp_fusion.2), kind=kCustom, calls=%fused_computation.clone.clone.1 | custom fusion | bytes 8388640 | tf_op jit(solution)/shard_map/while/body/eval_jaxpr/gather | solution.py:96
  87.4 4.7 %fusion.86 = (bf16[1024,1024]{1,0:T(8,128)(2,1)}, bf16[1024,1024]{1,0:T(8,128)(2,1)}) fusion(bf16[1024,2048]{1,0:T(8,128)(2,1)} %bitcast.95), kind=kLoop, calls=%fused_computation.60.clone.1 | loop fusion | bytes 8388608 | tf_op jit(solution)/shard_map/while/body/eval_jaxpr/slice | solution.py:97
  92.0 2.9 %copy.36 = bf16[1024,1024]{0,1:T(8,128)(2,1)S(1)} copy(bf16[1024,1024]{1,0:T(8,128)(2,1)} %get-tuple-element.252) | data formatting | bytes 4194304 | tf_op jit(solution)/shard_map/while
  97.1 3.3 %fusion.88 = (f32[16,64]{1,0:T(8,128)S(1)}, f32[16,64,1024]{2,1,0:T(8,128)}) fusion(f32[16,64,1024]{2,1,0:T(8,128)S(1)} %fusion.87, pred[1024]{0:T(1024)(128)(4,1)S(1)} %iota_compare_fusion.2), kind=kOutput, calls=%fused_computation.61.clone.1 | output fusion | flops 6292479 | bytes 8393728 | tf_op jit(solution)/shard_map/while/body/eval_jaxpr/sub | solution.py:71
  103.0 3.6 %fusion.89 = bf16[16,64,64]{2,1,0:T(8,128)(2,1)S(1)} fusion(bf16[1024,16,64]{0,2,1:T(8,128)(2,1)} %bitcast.97, f32[16,64,1024]{2,1,0:T(8,128)} %get-tuple-element.253, f32[16,64]{1,0:T(8,128)S(1)} %get-tuple-element.254), kind=kOutput, calls=%fused_computation.35.clone.1 | convolution fusion | flops 136380416 | bytes 6426624 | tf_op jit(solution)/shard_map/while/body/eval_jaxpr/hqk,khd->qhd/dot_general | solution.py:105
  111.2 3.6 %all-to-all-start = ((bf16[8,128,1024]{2,1,0:T(8,128)(2,1)}), bf16[8,128,1024]{2,1,0:T(8,128)(2,1)S(1)}, u32[]{:S(2)}, u32[]{:S(2)}) async-start(bf16[8,128,1024]{2,1,0:T(8,128)(2,1)} %broadcast_in_dim.65), calls=%async_computation | async-start | bytes 4194304 | tf_op jit(solution)/shard_map/all_to_all | solution.py:39
  116.0 25.9 %all-to-all-done = bf16[8,128,1024]{2,1,0:T(8,128)(2,1)S(1)} async-done(((bf16[8,128,1024]{2,1,0:T(8,128)(2,1)}), bf16[8,128,1024]{2,1,0:T(8,128)(2,1)S(1)}, u32[]{:S(2)}, u32[]{:S(2)}) %all-to-all-start) | async-done | bytes 2097184 | tf_op jit(solution)/shard_map/all_to_all | solution.py:39
  148.4 6.0 %collective-permute-start.3 = (bf16[512,256]{0,1:T(8,128)(2,1)S(1)}, bf16[512,256]{0,1:T(8,128)(2,1)S(1)}, u32[]{:S(2)}, u32[]{:S(2)}) collective-permute-start(bf16[512,256]{0,1:T(8,128)(2,1)S(1)} %get-tuple-element.168), channel_id=1, source_target_pairs={{8,0},{16,8},{24,16},{32,24},{40,32},{48,40},{56,48},{64,56},{72,6... | collective-permute-start | bytes 786440 | tf_op jit(solution)/shard_map/ppermute | solution.py:63
  156.0 4.6 %all-to-all-start.2 = ((bf16[8,128,1024]{2,1,0:T(8,128)(2,1)}), bf16[8,128,1024]{2,1,0:T(8,128)(2,1)}, u32[]{:S(2)}, u32[]{:S(2)}) async-start(bf16[8,128,1024]{2,1,0:T(8,128)(2,1)} %broadcast_in_dim.66), calls=%async_computation.2 | async-start | bytes 4194304 | tf_op jit(solution)/shard_map/all_to_all | solution.py:39
  161.8 18.3 %while.23 = (s32[]{:T(128)}, bf16[2,512,128]{2,1,0:T(8,128)(2,1)}, s32[2]{0:T(128)S(1)}, bf16[2048,256]{0,1:T(8,128)(2,1)S(1)}, s32[]{:T(128)}, /*index=5*/bf16[...) while((s32[]{:T(128)}, bf16[2,512,128]{2,1,0:T(8,128)(2,1)}, ...), condition=%wide.region_7.8_spmd, body=%wide.region_4.7_spmd.sunk | while | flops 621359104 | bytes 6319884 | solution.py:153
  180.1 7.4 %all-to-all-done.2 = bf16[8,128,1024]{2,1,0:T(8,128)(2,1)} async-done(((bf16[8,128,1024]{2,1,0:T(8,128)(2,1)}), bf16[8,128,1024]{2,1,0:T(8,128)(2,1)}, u32[]{:S(2)}, u32[]{:S(2)}) %all-to-all-start.2) | async-done | bytes 2097184 | tf_op jit(solution)/shard_map/all_to_all | solution.py:39
  187.6 10.8 %all_to_all.26 = bf16[8,128,128]{2,1,0:T(8,128)(2,1)S(1)} all-to-all(bf16[8,128,128]{2,1,0:T(8,128)(2,1)} %bitcast.14), channel_id=1, replica_groups=mesh['band'=32,'head'=8] {'head'}, dimensions={0} | all-to-all | bytes 524288 | tf_op jit(solution)/shard_map/all_to_all | solution.py:156
  198.4 2.7 %fusion.33 = bf16[128,1024]{1,0:T(8,128)(2,1)} fusion(bf16[8,128,1024]{2,1,0:T(8,128)(2,1)} %all-to-all-done.2, bf16[128,1024]{1,0:T(8,128)(2,1)S(1)} %fusion.34, bf16[8,128,128]{2,1,0:T(8,128)(2,1)S(1)} %all_to_all.26), kind=kOutput, calls=%fused_computation.54 | convolution fusion | flops 268828672 | bytes 2883584 | tf_op jit(solution)/shard_map/dot_general | solution.py:158
  (87 shorter events, 49.1 us)
Async XLA Ops:
  0.0 20.2 %copy-start = (bf16[1024,1024]{1,0:T(8,128)(2,1)S(1)}, bf16[1024,1024]{1,0:T(8,128)(2,1)}, u32[]{:S(2)}) copy-start(bf16[1024,1024]{1,0:T(8,128)(2,1)} %param.15) | copy-start | bytes 6291460
  2.6 18.1 %collective-permute-start = (bf16[2,131072]{1,0:T(2,128)(2,1)}, bf16[2,131072]{1,0:T(2,128)(2,1)S(1)}, u32[]{:S(2)}, u32[]{:S(2)}) collective-permute-start(bf16[2,131072]{1,0:T(2,128)(2,1)} %slice.48), channel_id=1, source_target_pairs={{0,1},{1,2},{2,3},{3,4},{4,5},{5,6},{6,7},{7,8},{8,9},{9,10},{10,1... | collective-permute-start | bytes 1572872 | tf_op jit(solution)/shard_map/ppermute | solution.py:25
  5.7 16.6 %collective-permute-start.1 = (bf16[2,131072]{1,0:T(2,128)(2,1)}, bf16[2,131072]{1,0:T(2,128)(2,1)}, u32[]{:S(2)}, u32[]{:S(2)}) collective-permute-start(bf16[2,131072]{1,0:T(2,128)(2,1)} %slice.50), channel_id=1, source_target_pairs={{1,0},{2,1},{3,2},{4,3},{5,4},{6,5},{7,6},{8,7},{9,8},{10,9},{11,1... | collective-permute-start | bytes 1572872 | tf_op jit(solution)/shard_map/ppermute | solution.py:26
  15.3 4.9 %copy-start.8 = (s32[2,8]{1,0:T(2,128)S(1)}, s32[2,8]{1,0:T(2,128)}, u32[]{:S(2)}) copy-start(s32[2,8]{1,0:T(2,128)} %param.20) | copy-start | bytes 196
  15.3 4.9 %copy-start.3 = (bf16[128,1024]{1,0:T(8,128)(2,1)S(1)}, bf16[128,1024]{1,0:T(8,128)(2,1)}, u32[]{:S(2)}) copy-start(bf16[128,1024]{1,0:T(8,128)(2,1)} %param.14) | copy-start | bytes 786436
  37.7 16.6 %copy-start.6 = (bf16[2,64,1024]{2,1,0:T(8,128)(2,1)S(1)}, bf16[2,64,1024]{2,1,0:T(8,128)(2,1)}, u32[]{:S(2)}) copy-start(bf16[2,64,1024]{2,1,0:T(8,128)(2,1)} %custom-call.3) | copy-start | bytes 786436
  37.7 16.6 %copy-start.9 = (s32[2]{0:T(128)S(1)}, s32[2]{0:T(128)}, u32[]{:S(2)}) copy-start(s32[2]{0:T(128)} %param.21) | copy-start | bytes 28
  70.8 3.3 %copy-start.2 = (bf16[1024,1024]{1,0:T(8,128)(2,1)S(1)}, bf16[1024,1024]{1,0:T(8,128)(2,1)}, u32[]{:S(2)}) copy-start(bf16[1024,1024]{1,0:T(8,128)(2,1)} %get-tuple-element.251) | copy-start | bytes 6291460 | tf_op jit(solution)/shard_map/while
  97.1 3.3 %copy-start.2 = (bf16[1024,1024]{1,0:T(8,128)(2,1)S(1)}, bf16[1024,1024]{1,0:T(8,128)(2,1)}, u32[]{:S(2)}) copy-start(bf16[1024,1024]{1,0:T(8,128)(2,1)} %get-tuple-element.251) | copy-start | bytes 6291460 | tf_op jit(solution)/shard_map/while
  106.7 0.7 copy-start.7
  109.6 5.2 %copy-start.4 = (bf16[3,1024,128]{2,1,0:T(8,128)(2,1)S(1)}, bf16[3,1024,128]{2,1,0:T(8,128)(2,1)}, u32[]{:S(2)}) copy-start(bf16[3,1024,128]{2,1,0:T(8,128)(2,1)} %param.18) | copy-start | bytes 2359300
  111.2 30.7 %all-to-all-start = ((bf16[8,128,1024]{2,1,0:T(8,128)(2,1)}), bf16[8,128,1024]{2,1,0:T(8,128)(2,1)S(1)}, u32[]{:S(2)}, u32[]{:S(2)}) async-start(bf16[8,128,1024]{2,1,0:T(8,128)(2,1)} %broadcast_in_dim.65), calls=%async_computation | async-start | bytes 4194304 | tf_op jit(solution)/shard_map/all_to_all | solution.py:39
  141.9 12.5 %copy-start.5 = (bf16[128,1024]{1,0:T(8,128)(2,1)S(1)}, bf16[128,1024]{1,0:T(8,128)(2,1)}, u32[]{:S(2)}) copy-start(bf16[128,1024]{1,0:T(8,128)(2,1)} %param.19) | copy-start | bytes 786436
  146.2 15.5 %collective-permute-start.2 = (bf16[512,256]{0,1:T(8,128)(2,1)S(1)}, bf16[512,256]{0,1:T(8,128)(2,1)S(1)}, u32[]{:S(2)}, u32[]{:S(2)}) collective-permute-start(bf16[512,256]{0,1:T(8,128)(2,1)S(1)} %get-tuple-element.167), channel_id=1, source_target_pairs={{0,8},{8,16},{16,24},{24,32},{32,40},{40,48},{48,56},{56,64},{64,7... | collective-permute-start | bytes 786440 | tf_op jit(solution)/shard_map/ppermute | solution.py:62
  148.4 13.3 %collective-permute-start.3 = (bf16[512,256]{0,1:T(8,128)(2,1)S(1)}, bf16[512,256]{0,1:T(8,128)(2,1)S(1)}, u32[]{:S(2)}, u32[]{:S(2)}) collective-permute-start(bf16[512,256]{0,1:T(8,128)(2,1)S(1)} %get-tuple-element.168), channel_id=1, source_target_pairs={{8,0},{16,8},{24,16},{32,24},{40,32},{48,40},{56,48},{64,56},{72,6... | collective-permute-start | bytes 786440 | tf_op jit(solution)/shard_map/ppermute | solution.py:63
  156.0 31.5 %all-to-all-start.2 = ((bf16[8,128,1024]{2,1,0:T(8,128)(2,1)}), bf16[8,128,1024]{2,1,0:T(8,128)(2,1)}, u32[]{:S(2)}, u32[]{:S(2)}) async-start(bf16[8,128,1024]{2,1,0:T(8,128)(2,1)} %broadcast_in_dim.66), calls=%async_computation.2 | async-start | bytes 4194304 | tf_op jit(solution)/shard_map/all_to_all | solution.py:39
  180.1 21.0 %copy-start.1 = (bf16[1024,1024]{1,0:T(8,128)(2,1)S(1)}, bf16[1024,1024]{1,0:T(8,128)(2,1)}, u32[]{:S(2)}) copy-start(bf16[1024,1024]{1,0:T(8,128)(2,1)} %param.15) | copy-start | bytes 6291460
where the time goes:
time: 202 us; the launch traced here: 201 us
  local copies, waits for them, and re-layouts  64.6 us (32%)
  matrix products  42.8 us (21%)
  waiting for transfers between devices  34.9 us (17%)
  starting transfers between devices  27.9 us (14%)
  other arithmetic  18.3 us (9%)
  blocking collectives  10.8 us (5%)
    all_to_all x2, waiting for transfers between devices, from_everyone(): lax.all_to_all(jnp.broadcast_to(shard[None], (size, *shard.shape)), axis,...  33.3 us
    dot_general x1, matrix products, local(): jnp.dot(bordered.reshape(-1, model_width), enc_keyval, preferred_element_...  16.6 us
    gather x2, local copies, waits for them, and re-layouts, one_tile(): gathered = grid_tiles[tile_list].reshape(LIST * GT, 2 * model_width)  13.7 us
    while x8, local copies, waits for them, and re-layouts  10.8 us
    all_to_all x1, blocking collectives, local(): lax.all_to_all(proc_attn, 'head', split_axis=0, concat_axis=1, tiled=True)  10.8 us
    ppermute x1, starting transfers between devices, padded(): lax.ppermute(first, axis, [(b, a) for a, b in up])  9.57 us
    slice x2, local copies, waits for them, and re-layouts, one_tile(): key_rows = gathered[:, :model_width].reshape(LIST * GT, HEADS, head_size)  9.31 us
    reshape x1, local copies, waits for them, and re-layouts, local(): bordered.reshape(-1, model_width)  8.2 us
  transfers between devices with their start and end apart: 6, of which 3 were waited for; matrix products, arithmetic and copies ran while one was open for 14% of the time, Pallas kernels for 0%

commit v1 on v0

v1 whole, which is shorter than its diff:
```python
import jax
import jax.numpy as jnp
from jax import lax
from jax.experimental import pallas as pl
from jax.experimental.pallas import tpu as pltpu
from jax.sharding import PartitionSpec as P

D = 1024
HEADS = 16
HD = D // HEADS
HALFW = 512
GT = 128
LIST = 8
MT = 64
HALO = 2
BF = jnp.bfloat16
F32 = jnp.float32
NEG = -1e30
SCALE = HD**-0.5
VM = pltpu.VMEM
CP = pltpu.make_async_copy


def dot(a, b):
    return jnp.dot(a, b, preferred_element_type=F32)


def dot_t(a, b):
    return lax.dot_general(a, b, (((1,), (1,)), ((), ())), preferred_element_type=F32)


def spread(q, heads):
    n, w = q.shape
    rows = lax.broadcasted_iota(jnp.int32, (heads * n, w), 0) // n
    cols = lax.broadcasted_iota(jnp.int32, (heads * n, w), 1) // HD
    tall = jnp.concatenate([q.astype(F32) * SCALE] * heads, axis=0)
    return jnp.where(rows == cols, tall, 0.0).astype(BF)


def collect(o, heads):
    n, w = o.shape[0] // heads, o.shape[1]
    cols = lax.broadcasted_iota(jnp.int32, (n, w), 1) // HD
    total = o[:n]
    for h in range(1, heads):
        total = jnp.where(cols == h, o[h * n : (h + 1) * n], total)
    return total


KV_ROWS = 512
KV_COLS = 512


def own_kv_body(x_hbm, w_hbm, out_hbm, xb, wb, ob, sx, sw, so):
    rows, cols = x_hbm.shape[0] // KV_ROWS, w_hbm.shape[1] // KV_COLS

    def x_copy(m):
        at = pl.ds(m * KV_ROWS, KV_ROWS)
        return CP(x_hbm.at[at], xb.at[at], sx.at[m])

    def w_copy(n):
        at = pl.ds(n * KV_COLS, KV_COLS)
        return CP(w_hbm.at[:, at], wb.at[:, at], sw.at[n])

    def o_copy(m):
        at = pl.ds(m * KV_ROWS, KV_ROWS)
        return CP(ob.at[at], out_hbm.at[at], so.at[m])

    x_copy(0).start()
    for n in range(cols):
        w_copy(n).start()
    for m in range(1, rows):
        x_copy(m).start()

    def step(m, carry):
        at = pl.ds(pl.multiple_of(m * KV_ROWS, KV_ROWS), KV_ROWS)
        x_copy(m).wait()
        x = xb[at, :]
        for n in range(cols):

            @pl.when(m == 0)
            def _():
                w_copy(n).wait()

            cut = slice(n * KV_COLS, (n + 1) * KV_COLS)
            ob[at, cut] = dot(x, wb[:, cut]).astype(BF)
        o_copy(m).start()
        return carry

    lax.fori_loop(0, rows, step, 0)
    for m in range(rows):
        o_copy(m).wait()


def own_kv(x, w):
    rows, cols = x.shape[0] // KV_ROWS, w.shape[1] // KV_COLS
    hbm = pl.BlockSpec(memory_space=pltpu.HBM)
    return pl.pallas_call(
        own_kv_body,
        out_shape=jax.ShapeDtypeStruct((x.shape[0], w.shape[1]), BF),
        in_specs=[hbm, hbm],
        out_specs=hbm,
        scratch_shapes=[
            VM(x.shape, BF),
            VM(w.shape, BF),
            VM((x.shape[0], w.shape[1]), BF),
            pltpu.SemaphoreType.DMA((rows,)),
            pltpu.SemaphoreType.DMA((cols,)),
            pltpu.SemaphoreType.DMA((rows,)),
        ],
        cost_estimate=pl.CostEstimate(
            flops=2 * x.shape[0] * w.shape[0] * w.shape[1],
            transcendentals=0,
            bytes_accessed=2 * (x.size + w.size + x.shape[0] * w.shape[1]),
        ),
        name="own_kv",
    )(x, w)


def encode_body(
    ids, counts, kv_hbm, lo_hbm, hi_hbm, w_hbm, mf, wq_hbm, wo_hbm, out, kv, xh, wb, wq, wo, qs, at_s, sem, sw
):
    tiles = kv_hbm.shape[0]
    hr = HALO * GT
    cols = w_hbm.shape[1] // KV_COLS
    c_lo = CP(lo_hbm, xh.at[pl.ds(0, hr)], sem.at[0])
    c_hi = CP(hi_hbm, xh.at[pl.ds(hr, hr)], sem.at[1])
    c_wq = CP(wq_hbm, wq, sem.at[2])
    c_kv = CP(kv_hbm, kv.at[pl.ds(HALO, tiles)], sem.at[3])
    c_wo = CP(wo_hbm, wo, sem.at[4])

    def w_copy(n):
        at = pl.ds(n * KV_COLS, KV_COLS)
        return CP(w_hbm.at[:, at], wb.at[:, at], sw.at[n])

    c_wq.start()
    c_lo.start()
    c_hi.start()
    for n in range(cols):
        w_copy(n).start()
    c_kv.start()
    c_wo.start()
    c_wq.wait()
    qs[...] = dot(mf[...], wq[...]).astype(BF)
    c_lo.wait()
    c_hi.wait()
    for n in range(cols):
        w_copy(n).wait()
        cut = slice(n * KV_COLS, (n + 1) * KV_COLS)
        r = dot(xh[...], wb[:, cut]).astype(BF)
        for t in range(HALO):
            kv[t, :, cut] = r[t * GT : (t + 1) * GT]
            kv[HALO + tiles + t, :, cut] = r[hr + t * GT : hr + (t + 1) * GT]
    first = lax.axis_index(("band", "head")) * tiles - HALO
    c_kv.wait()
    c_wo.wait()
    gw = 4 * HD

    for m in range(mf.shape[0] // MT):
        valid = counts[m]
        at = [ids[m, s] - first for s in range(LIST)]

        for g in range(D // gw):
            q = spread(qs[m * MT : (m + 1) * MT, g * gw : (g + 1) * gw], 4)
            parts = []
            for j in range(LIST // 2):
                k = jnp.concatenate([kv[at[2 * j + i], :, g * gw : (g + 1) * gw] for i in range(2)], axis=0)
                s = dot_t(q, k)
                pos = lax.broadcasted_iota(jnp.int32, s.shape, 1) + 2 * j * GT
                parts.append(jnp.where(pos < valid, s, NEG))
            s = jnp.concatenate(parts, axis=1)
            p = jnp.exp(s - jnp.max(s, axis=1, keepdims=True))
            total = jnp.sum(p, axis=1, keepdims=True)
            p = p.astype(BF)
            o = None
            for j in range(LIST // 2):
                v = jnp.concatenate(
                    [kv[at[2 * j + i], :, D + g * gw : D + (g + 1) * gw] for i in range(2)], axis=0
                )
                part = dot(p[:, 2 * j * GT : 2 * (j + 1) * GT], v)
                o = part if o is None else o + part
            at_s[m * MT : (m + 1) * MT, g * gw : (g + 1) * gw] = collect(o / total, 4).astype(BF)
    out[...] = (mf[...].astype(F32) + dot(at_s[...], wo[...])).astype(BF)


def encode(ids, counts, kv_own, lo, hi, w, mf, wq, wo):
    hbm = pl.BlockSpec(memory_space=pltpu.HBM)
    vm = pl.BlockSpec(memory_space=pltpu.VMEM)
    sm = pl.BlockSpec(memory_space=pltpu.SMEM)
    tiles = kv_own.shape[0]
    return pl.pallas_call(
        encode_body,
        out_shape=jax.ShapeDtypeStruct(mf.shape, BF),
        in_specs=[sm, sm, hbm, hbm, hbm, hbm, vm, hbm, hbm],
        out_specs=vm,
        scratch_shapes=[
            VM((tiles + 2 * HALO, GT, 2 * D), BF),
            VM((2 * HALO * GT, D), BF),
            VM(w.shape, BF),
            VM(wq.shape, BF),
            VM(wo.shape, BF),
            VM(mf.shape, BF),
            VM(mf.shape, BF),
            pltpu.SemaphoreType.DMA((5,)),
            pltpu.SemaphoreType.DMA((w.shape[1] // KV_COLS,)),
        ],
        cost_estimate=pl.CostEstimate(flops=12 * 10**9, transcendentals=2 * 10**6, bytes_accessed=16 * 2**20),
        name="encode",
    )(ids, counts, kv_own, lo, hi, w, mf, wq, wo)


def sources(h):
    n = lax.axis_size("head")
    p = h ^ 1
    return [h, (h + n - 2) % n, (h + 2) % n, (h + 4) % n, p, (p + n - 2) % n, (p + 2) % n, (p + 4) % n]


def ring_exchange(x):
    n = lax.axis_size("head")
    right = [(i, (i + 2) % n) for i in range(n)]
    left = [(i, (i - 2) % n) for i in range(n)]
    flip = [(i, i ^ 1) for i in range(n)]
    half = x.shape[0] // 2
    r1 = lax.ppermute(x, "head", right)
    l1 = lax.ppermute(x, "head", left)
    o0 = lax.ppermute(x, "head", flip)
    a = lax.ppermute(r1[:half], "head", right)
    b = lax.ppermute(l1[half:], "head", left)
    o1 = lax.ppermute(jnp.concatenate([r1, l1], axis=0), "head", flip)
    o2 = lax.ppermute(jnp.concatenate([a, b], axis=0), "head", flip)
    return [x, r1, l1, a, b, o0, o1, o2]


def gather_rows(refs):
    x, r1, l1, a, b, o0, o1, o2 = refs
    return jnp.concatenate([r[...] for r in (x, r1, l1, a, b, o0, o1, o2)], axis=0)


def qkv_body(x, r1, l1, a, b, o0, o1, o2, w, q_out, kva, kvb, kv):
    rows = gather_rows((x, r1, l1, a, b, o0, o1, o2))
    n = x.shape[0]
    wqk = jnp.concatenate([w[0], w[1]], axis=1)
    qk = dot(rows, wqk).astype(BF)
    v = dot(rows, w[2]).astype(BF)
    hc = w.shape[2]
    for i, place in enumerate(sources(lax.axis_index("head"))):
        at = pl.ds(pl.multiple_of(place * n, n), n)
        q_out[at, :] = qk[i * n : (i + 1) * n, :hc]
        kv[at, :hc] = qk[i * n : (i + 1) * n, hc:]
        kv[at, hc:] = v[i * n : (i + 1) * n]
    half = kva.shape[0]
    kva[...] = kv[:half]
    kvb[...] = kv[half:]


def project_qkv(pieces, w):
    n, hc = pieces[0].shape[0], w.shape[2]
    group = n * lax.axis_size("head")
    half = jax.ShapeDtypeStruct((group // 2, 2 * hc), BF)
    return pl.pallas_call(
        qkv_body,
        out_shape=(jax.ShapeDtypeStruct((group, hc), BF), half, half),
        scratch_shapes=[VM((group, 2 * hc), BF)],
        cost_estimate=pl.CostEstimate(flops=6 * group * D * hc, transcendentals=0, bytes_accessed=4 * 2**20),
        name="qkv",
    )(*pieces, w)


QB = 128


def window_body(q, lo, kva, kvb, hi, out, kv):
    hc = q.shape[1]
    heads = hc // HD
    for i, r in enumerate((lo, kva, kvb, hi)):
        kv[i * HALFW : (i + 1) * HALFW] = r[...]
    band = lax.axis_index("band")
    bands = lax.axis_size("band")
    has_lo = band > 0
    has_hi = band < bands - 1
    side = HALFW // QB
    blocks = q.shape[0] // QB
    row = lax.broadcasted_iota(jnp.int32, (heads * QB, QB), 0) % QB
    col = lax.broadcasted_iota(jnp.int32, (heads * QB, QB), 1)
    for n in range(blocks):
        qn = spread(q[n * QB : (n + 1) * QB], heads)
        span = slice(n * QB, (n + 2 * side + 1) * QB)
        s = dot_t(qn, kv[span, :hc])
        parts = []
        for c in range(2 * side + 1):
            part = s[:, c * QB : (c + 1) * QB]
            ok = None
            if c == 0:
                ok = col > row
            if c == 2 * side:
                ok = col < row
            if n + c < side:
                ok = has_lo if ok is None else jnp.logical_and(ok, has_lo)
            if n + c >= side + blocks:
                ok = has_hi if ok is None else jnp.logical_and(ok, has_hi)
            parts.append(part if ok is None else jnp.where(ok, part, NEG))
        s = jnp.concatenate(parts, axis=1)
        p = jnp.exp(s - jnp.max(s, axis=1, keepdims=True))
        total = jnp.sum(p, axis=1, keepdims=True)
        o = dot(p.astype(BF), kv[span, hc:])
        out[n] = collect(o / total, heads).astype(BF)


def window(q, lo, kva, kvb, hi):
    group, hc = q.shape
    return pl.pallas_call(
        window_body,
        out_shape=jax.ShapeDtypeStruct((group // QB, QB, hc), BF),
        scratch_shapes=[VM((group + 2 * HALFW, 2 * hc), BF)],
        cost_estimate=pl.CostEstimate(flops=2 * 10**9, transcendentals=2 * 10**6, bytes_accessed=2 * 2**20),
        name="window",
    )(q, lo, kva, kvb, hi)


def finish_body(at, ms, x, r1, l1, a, b, o0, o1, o2, out):
    rows = gather_rows((x, r1, l1, a, b, o0, o1, o2))
    att = jnp.concatenate([at[place] for place in sources(lax.axis_index("head"))], axis=1)
    out[...] = (ms[...].astype(F32) + dot(att, rows)).astype(BF)


def finish(attn, state, pieces):
    return pl.pallas_call(
        finish_body,
        out_shape=jax.ShapeDtypeStruct(state.shape, BF),
        cost_estimate=pl.CostEstimate(flops=2 * state.size * D, transcendentals=0, bytes_accessed=3 * 2**20),
        name="finish",
    )(attn, state, *pieces)


def local(grid_feat, mesh_feat, enc_query, enc_keyval, enc_out, proc_qkv, proc_out, tile_ids, key_counts):
    tiles = grid_feat.shape[0] // GT
    both = ("band", "head")
    size = lax.axis_size(both)
    up = [(i, i + 1) for i in range(size - 1)]
    down = [(b, a) for a, b in up]
    lo = lax.ppermute(grid_feat[-HALO * GT :], both, up)
    hi = lax.ppermute(grid_feat[: HALO * GT], both, down)
    out_pieces = ring_exchange(proc_out)
    kv_own = own_kv(grid_feat, enc_keyval).reshape(tiles, GT, 2 * D)
    state = encode(tile_ids, key_counts, kv_own, lo, hi, enc_keyval, mesh_feat, enc_query, enc_out)
    q, kva, kvb = project_qkv(ring_exchange(state), proc_qkv)
    bands = lax.axis_size("band")
    b_up = [(i, i + 1) for i in range(bands - 1)]
    b_down = [(b, a) for a, b in b_up]
    k_lo = lax.ppermute(kvb, "band", b_up)
    k_hi = lax.ppermute(kva, "band", b_down)
    attn = window(q, k_lo, kva, kvb, k_hi)
    attn = lax.all_to_all(attn, "head", split_axis=0, concat_axis=0, tiled=True)
    return finish(attn, state, out_pieces)


def solution(mesh):
    rows = P(("band", "head"), None)
    return jax.shard_map(
        local,
        mesh=mesh,
        in_specs=(
            rows,
            rows,
            P(),
            P(),
            P(),
            P(None, None, "head"),
            P("head", None),
            rows,
            P(("band", "head")),
        ),
        out_specs=rows,
        check_vma=False,
    )
```

time: 202 us -> 103 us (0.51)
  local copies, waits for them, and re-layouts: 64.6 us -> 5.22 us
  matrix products: 42.8 us -> 0 us
  Pallas kernels: 0 us -> 39.8 us
  other arithmetic: 18.3 us -> 0.11 us
  waiting for transfers between devices: 34.9 us -> 21.8 us
  blocking collectives: 10.8 us -> 0 us
  starting transfers between devices: 27.9 us -> 35.3 us
    pallas_call x0 -> x5, Pallas kernels: none -> 39.8 us  [the longest x1 14.6 us: own_kv(): pl.pallas_call(own_kv_body, out_shape=jax.ShapeDtypeStruct((x.shape[0], w...]
    dot_general x10 -> x0, matrix products: 35.8 us -> none  [the longest x1 16.6 us: local(): jnp.dot(bordered.reshape(-1, model_width), enc_keyval, preferred_element_...]
    all_to_all x2 -> x1, waiting for transfers between devices: 33.3 us -> 7.37 us  [local(): attn = lax.all_to_all(attn, 'head', split_axis=0, concat_axis=0, tiled=True)]
    slice x11 -> x5, local copies, waits for them, and re-layouts: 17.2 us -> 1.31 us  [the longest x1 1.27 us: local(): hi = lax.ppermute(grid_feat[:HALO * GT], both, down)]
    gather x2 -> x0, local copies, waits for them, and re-layouts: 13.7 us -> none  [one_tile(): gathered = grid_tiles[tile_list].reshape(LIST * GT, 2 * model_width)]
    reshape x4 -> x0, local copies, waits for them, and re-layouts: 13.5 us -> none  [the longest x1 8.2 us: local(): bordered.reshape(-1, model_width)]
    ppermute x4 -> x18, waiting for transfers between devices: 1.58 us -> 14.5 us  [the longest x2 6.74 us: ring_exchange(): a = lax.ppermute(r1[:half], 'head', right)]
    ppermute x4 -> x18, starting transfers between devices: 19.7 us -> 31.9 us  [the longest x1 9.58 us: local(): hi = lax.ppermute(grid_feat[:HALO * GT], both, down)]
  transfers between devices with their start and end apart: 6 -> 19, of which waited for: 3 -> 5; matrix products, arithmetic and copies ran while one was open for 14% -> 0% of each run, Pallas kernels for 0% -> 25%
where the time goes in v1:
time: 103 us
  Pallas kernels  39.8 us (39%)
  starting transfers between devices  35.3 us (34%)
  waiting for transfers between devices  21.8 us (21%)
  local copies, waits for them, and re-layouts  5.22 us (5%)
    pallas_call x1, Pallas kernels, own_kv(): pl.pallas_call(own_kv_body, out_shape=jax.ShapeDtypeStruct((x.shape[0], w...  14.6 us
    pallas_call x1, Pallas kernels, encode(): pl.pallas_call(encode_body, out_shape=jax.ShapeDtypeStruct(mf.shape, BF),...  11.7 us
    ppermute x1, starting transfers between devices, local(): hi = lax.ppermute(grid_feat[:HALO * GT], both, down)  9.58 us
    all_to_all x1, waiting for transfers between devices, local(): attn = lax.all_to_all(attn, 'head', split_axis=0, concat_axis=0, tiled=True)  7.37 us
    ppermute x2, waiting for transfers between devices, ring_exchange(): a = lax.ppermute(r1[:half], 'head', right)  6.74 us
    pallas_call x1, Pallas kernels, window(): pl.pallas_call(window_body, out_shape=jax.ShapeDtypeStruct((group // QB,...  6.7 us
    ppermute x2, starting transfers between devices, ring_exchange(): b = lax.ppermute(l1[half:], 'head', left)  6.59 us
    ppermute x2, starting transfers between devices, ring_exchange(): l1 = lax.ppermute(x, 'head', left)  5.24 us
  transfers between devices with their start and end apart: 19, of which 5 were waited for; matrix products, arithmetic and copies ran while one was open for 0% of the time, Pallas kernels for 25%

profile of v1, /device:TPU:24, one launch (start us, length us, event | category | flops | bytes accessed | tf_op | source)
XLA Modules:
  0.0 102.6 jit_solution(2236493729174737572)
XLA Ops:
  0.0 1.3 %fusion = (bf16[256,1024]{1,0:T(8,128)(2,1)S(1)}, bf16[256,1024]{1,0:T(8,128)(2,1)S(1)}) fusion(bf16[2048,1024]{1,0:T(8,128)(2,1)} %x_hbm.1), kind=kLoop, calls=%fused_computation.4 | loop fusion | bytes 2097152 | tf_op jit(solution)/shard_map/slice | solution.py:341
  1.3 1.9 %collective-permute-start = (bf16[256,1024]{1,0:T(8,128)(2,1)S(1)}, bf16[256,1024]{1,0:T(8,128)(2,1)S(1)}, u32[]{:S(2)}, u32[]{:S(2)}) collective-permute-start(bf16[256,1024]{1,0:T(8,128)(2,1)S(1)} %get-tuple-element.12), channel_id=1, source_target_pairs={{0,1},{1,2},{2,3},{3,4},{4,5},{5,6},{6,7},{7,8},{8,9},{9,10},{10,1... | collective-permute-start | bytes 1572872 | tf_op jit(solution)/shard_map/ppermute | solution.py:340
  3.2 9.6 %collective-permute-start.1 = (bf16[256,1024]{1,0:T(8,128)(2,1)S(1)}, bf16[256,1024]{1,0:T(8,128)(2,1)S(1)}, u32[]{:S(2)}, u32[]{:S(2)}) collective-permute-start(bf16[256,1024]{1,0:T(8,128)(2,1)S(1)} %get-tuple-element.11), channel_id=1, source_target_pairs={{1,0},{2,1},{3,2},{4,3},{5,4},{6,5},{7,6},{8,7},{9,8},{10,9},{11,1... | collective-permute-start | bytes 1572872 | tf_op jit(solution)/shard_map/ppermute | solution.py:341
  12.8 14.6 %own_kv.1 = bf16[2048,2048]{1,0:T(8,128)(2,1)} custom-call(bf16[2048,1024]{1,0:T(8,128)(2,1)} %x_hbm.1, bf16[1024,2048]{1,0:T(8,128)(2,1)} %w_hbm.3), custom_call_target="tpu_custom_call" | custom-call | flops 8589934592 | bytes 16777216 | tf_op jit(solution)/shard_map/own_kv/pallas_call | solution.py:97
  27.5 0.8 copy-done.14
  28.4 11.7 %encode.1.x.ms = bf16[128,1024]{1,0:T(8,128)(2,1)} custom-call(s32[2,8]{1,0:T(2,128)} %ids.1, s32[2]{0:T(128)} %counts.1, bf16[16,128,2048]{2,1,0:T(8,128)(2,1)} %bitcast.1, bf16[256,1024]{1,0:T(8,128)(2,1)} %copy-done.14, bf16[256,1024]{1,0:T(8,128)(2,1)} %copy-done.15, bf16[1024,2048]{1,0:T(8,128)(2,1)} %w_hbm.3, bf16[128,1024]{1,0:T(8,128)(2,1)} %mf.1, ...), custom_call_target="tpu_custom_call" | custom-call | flops 12000000000 | bytes 16777216 | tf_op jit(solution)/shard_map/encode/pallas_call | solution.py:190
  40.2 3.2 %collective-permute-start.3 = (bf16[128,1024]{1,0:T(8,128)(2,1)}, bf16[128,1024]{1,0:T(8,128)(2,1)S(1)}, u32[]{:S(2)}, u32[]{:S(2)}) collective-permute-start(bf16[128,1024]{1,0:T(8,128)(2,1)} %encode.1.x.ms), channel_id=1, source_target_pairs={{0,6},{1,7},{2,0},{3,1},{4,2},{5,3},{6,4},{7,5},{8,14},{9,15},{10,... | collective-permute-start | bytes 786440 | tf_op jit(solution)/shard_map/ppermute | solution.py:224
  43.5 4.6 %collective-permute-done.2.r1 = bf16[128,1024]{1,0:T(8,128)(2,1)S(1)} collective-permute-done((bf16[128,1024]{1,0:T(8,128)(2,1)}, bf16[128,1024]{1,0:T(8,128)(2,1)S(1)}, u32[]{:S(2)}, u32[]{:S(2)}) %collective-permute-start.2) | collective-permute-done | bytes 262176 | tf_op jit(solution)/shard_map/ppermute | solution.py:223
  48.3 3.3 %collective-permute-start.5 = (bf16[64,1024]{1,0:T(8,128)(2,1)S(1)}, bf16[64,1024]{1,0:T(8,128)(2,1)S(1)}, u32[]{:S(2)}, u32[]{:S(2)}) collective-permute-start(bf16[64,1024]{1,0:T(8,128)(2,1)S(1)} %slice.25), channel_id=1, source_target_pairs={{0,6},{1,7},{2,0},{3,1},{4,2},{5,3},{6,4},{7,5},{8,14},{9,15},{10,... | collective-permute-start | bytes 393224 | tf_op jit(solution)/shard_map/ppermute | solution.py:227
  51.8 3.8 %collective-permute-done.4.a = bf16[64,1024]{1,0:T(8,128)(2,1)S(1)} collective-permute-done((bf16[64,1024]{1,0:T(8,128)(2,1)S(1)}, bf16[64,1024]{1,0:T(8,128)(2,1)S(1)}, u32[]{:S(2)}, u32[]{:S(2)}) %collective-permute-start.4) | collective-permute-done | bytes 131104 | tf_op jit(solution)/shard_map/ppermute | solution.py:226
  55.8 1.3 %collective-permute-start.11 = (bf16[128,1024]{1,0:T(8,128)(2,1)S(1)}, bf16[128,1024]{1,0:T(8,128)(2,1)S(1)}, u32[]{:S(2)}, u32[]{:S(2)}) collective-permute-start(bf16[128,1024]{1,0:T(8,128)(2,1)S(1)} %copy-done.8), channel_id=1, source_target_pairs={{0,2},{1,3},{2,4},{3,5},{4,6},{5,7},{6,0},{7,1},{8,10},{9,11},{10,... | collective-permute-start | bytes 786440 | tf_op jit(solution)/shard_map/ppermute | solution.py:223
  57.1 2.0 %collective-permute-start.12 = (bf16[128,1024]{1,0:T(8,128)(2,1)S(1)}, bf16[128,1024]{1,0:T(8,128)(2,1)S(1)}, u32[]{:S(2)}, u32[]{:S(2)}) collective-permute-start(bf16[128,1024]{1,0:T(8,128)(2,1)S(1)} %copy-done.8), channel_id=1, source_target_pairs={{0,6},{1,7},{2,0},{3,1},{4,2},{5,3},{6,4},{7,5},{8,14},{9,15},{10,... | collective-permute-start | bytes 786440 | tf_op jit(solution)/shard_map/ppermute | solution.py:224
  59.9 0.8 copy-done.13
  60.7 3.9 %qkv.1 = (bf16[1024,128]{1,0:T(8,128)(2,1)}, bf16[512,256]{1,0:T(8,128)(2,1)}, bf16[512,256]{1,0:T(8,128)(2,1)}) custom-call(bf16[128,1024]{1,0:T(8,128)(2,1)} %encode.1.x.ms, bf16[128,1024]{1,0:T(8,128)(2,1)} %copy-done.3, bf16[128,1024]{1,0:T(8,128)(2,1)} %copy-done.4, bf16[64,1024]{1,0:T(8,128)(2,1)} %copy-done.11, bf16[64,1024]{1,0:T(8,128)(2,1)} %copy-done.12, ...), custom_call_target="tpu_custom_call" | custom-call | flops 805306368 | bytes 4194304 | tf_op jit(solution)/shard_map/qkv/pallas_call | solution.py:259
  64.6 4.1 %collective-permute-start.10 = (bf16[512,256]{1,0:T(8,128)(2,1)}, bf16[512,256]{1,0:T(8,128)(2,1)S(1)}, u32[]{:S(2)}, u32[]{:S(2)}) collective-permute-start(bf16[512,256]{1,0:T(8,128)(2,1)} %get-tuple-element.10.kva), channel_id=1, source_target_pairs={{8,0},{16,8},{24,16},{32,24},{40,32},{48,40},{56,48},{64,56},{72,6... | collective-permute-start | bytes 786440 | tf_op jit(solution)/shard_map/ppermute | solution.py:350
  68.7 1.9 %collective-permute-start.9 = (bf16[512,256]{1,0:T(8,128)(2,1)}, bf16[512,256]{1,0:T(8,128)(2,1)S(1)}, u32[]{:S(2)}, u32[]{:S(2)}) collective-permute-start(bf16[512,256]{1,0:T(8,128)(2,1)} %get-tuple-element.9.kvb), channel_id=1, source_target_pairs={{0,8},{8,16},{16,24},{24,32},{32,40},{40,48},{48,56},{56,64},{64,7... | collective-permute-start | bytes 786440 | tf_op jit(solution)/shard_map/ppermute | solution.py:349
  70.8 3.3 %collective-permute-start.14 = (bf16[64,1024]{1,0:T(8,128)(2,1)S(1)}, bf16[64,1024]{1,0:T(8,128)(2,1)S(1)}, u32[]{:S(2)}, u32[]{:S(2)}) collective-permute-start(bf16[64,1024]{1,0:T(8,128)(2,1)S(1)} %slice.27), channel_id=1, source_target_pairs={{0,6},{1,7},{2,0},{3,1},{4,2},{5,3},{6,4},{7,5},{8,14},{9,15},{10,... | collective-permute-start | bytes 393224 | tf_op jit(solution)/shard_map/ppermute | solution.py:227
  74.1 2.9 %collective-permute-done.13.a = bf16[64,1024]{1,0:T(8,128)(2,1)S(1)} collective-permute-done((bf16[64,1024]{1,0:T(8,128)(2,1)S(1)}, bf16[64,1024]{1,0:T(8,128)(2,1)S(1)}, u32[]{:S(2)}, u32[]{:S(2)}) %collective-permute-start.13) | collective-permute-done | bytes 131104 | tf_op jit(solution)/shard_map/ppermute | solution.py:226
  77.7 3.1 %collective-permute-done.9.lo = bf16[512,256]{1,0:T(8,128)(2,1)S(1)} collective-permute-done((bf16[512,256]{1,0:T(8,128)(2,1)}, bf16[512,256]{1,0:T(8,128)(2,1)S(1)}, u32[]{:S(2)}, u32[]{:S(2)}) %collective-permute-start.9) | collective-permute-done | bytes 262176 | tf_op jit(solution)/shard_map/ppermute | solution.py:349
  80.8 0.7 copy-done.17
  81.5 6.7 %window.1 = bf16[8,128,128]{2,1,0:T(8,128)(2,1)} custom-call(bf16[1024,128]{1,0:T(8,128)(2,1)} %get-tuple-element.8.q, bf16[512,256]{1,0:T(8,128)(2,1)} %copy-done.17, bf16[512,256]{1,0:T(8,128)(2,1)} %get-tuple-element.10.kva, bf16[512,256]{1,0:T(8,128)(2,1)} %get-tuple-element.9.kvb, bf16[512,256]{1,0:T(8,128)(2,1)} %copy-done.16), custom_call_target="tpu_custom_call" | custom-call | flops 2000000000 | bytes 2097152 | tf_op jit(solution)/shard_map/window/pallas_call | solution.py:310
  88.2 3.4 %all-to-all-start = ((bf16[8,128,128]{2,1,0:T(8,128)(2,1)}), bf16[8,128,128]{2,1,0:T(8,128)(2,1)S(1)}, u32[]{:S(2)}, u32[]{:S(2)}) async-start(bf16[8,128,128]{2,1,0:T(8,128)(2,1)} %window.1), calls=%async_computation | async-start | bytes 524288 | tf_op jit(solution)/shard_map/all_to_all | solution.py:352
  91.7 7.4 %all-to-all-done.at = bf16[8,128,128]{2,1,0:T(8,128)(2,1)S(1)} async-done(((bf16[8,128,128]{2,1,0:T(8,128)(2,1)}), bf16[8,128,128]{2,1,0:T(8,128)(2,1)S(1)}, u32[]{:S(2)}, u32[]{:S(2)}) %all-to-all-start) | async-done | bytes 262176 | tf_op jit(solution)/shard_map/all_to_all | solution.py:352
  99.8 2.8 %finish.1 = bf16[128,1024]{1,0:T(8,128)(2,1)} custom-call(bf16[8,128,128]{2,1,0:T(8,128)(2,1)} %copy-done.2, bf16[128,1024]{1,0:T(8,128)(2,1)} %encode.1.x.ms, bf16[128,1024]{1,0:T(8,128)(2,1)} %x.1, bf16[128,1024]{1,0:T(8,128)(2,1)} %copy-done, bf16[128,1024]{1,0:T(8,128)(2,1)} %copy-done.1, bf16[64,1024]{1,0:T(8,128)(2,1)} %copy-done.5, ...), custom_call_target="tpu_custom_call" | custom-call | flops 268435456 | bytes 3145728 | tf_op jit(solution)/shard_map/finish/pallas_call | solution.py:326
  (68 shorter events, 3.1 us)
Async XLA Ops:
  1.3 26.2 %collective-permute-start = (bf16[256,1024]{1,0:T(8,128)(2,1)S(1)}, bf16[256,1024]{1,0:T(8,128)(2,1)S(1)}, u32[]{:S(2)}, u32[]{:S(2)}) collective-permute-start(bf16[256,1024]{1,0:T(8,128)(2,1)S(1)} %get-tuple-element.12), channel_id=1, source_target_pairs={{0,1},{1,2},{2,3},{3,4},{4,5},{5,6},{6,7},{7,8},{8,9},{9,10},{10,1... | collective-permute-start | bytes 1572872 | tf_op jit(solution)/shard_map/ppermute | solution.py:340
  3.2 24.3 %collective-permute-start.1 = (bf16[256,1024]{1,0:T(8,128)(2,1)S(1)}, bf16[256,1024]{1,0:T(8,128)(2,1)S(1)}, u32[]{:S(2)}, u32[]{:S(2)}) collective-permute-start(bf16[256,1024]{1,0:T(8,128)(2,1)S(1)} %get-tuple-element.11), channel_id=1, source_target_pairs={{1,0},{2,1},{3,2},{4,3},{5,4},{6,5},{7,6},{8,7},{9,8},{10,9},{11,1... | collective-permute-start | bytes 1572872 | tf_op jit(solution)/shard_map/ppermute | solution.py:341
  28.4 27.3 %copy-start.8 = (bf16[128,1024]{1,0:T(8,128)(2,1)S(1)}, bf16[128,1024]{1,0:T(8,128)(2,1)}, u32[]{:S(2)}) copy-start(bf16[128,1024]{1,0:T(8,128)(2,1)} %x.1) | copy-start | bytes 786436
  40.1 7.9 %collective-permute-start.2 = (bf16[128,1024]{1,0:T(8,128)(2,1)}, bf16[128,1024]{1,0:T(8,128)(2,1)S(1)}, u32[]{:S(2)}, u32[]{:S(2)}) collective-permute-start(bf16[128,1024]{1,0:T(8,128)(2,1)} %encode.1.x.ms), channel_id=1, source_target_pairs={{0,2},{1,3},{2,4},{3,5},{4,6},{5,7},{6,0},{7,1},{8,10},{9,11},{10,... | collective-permute-start | bytes 786440 | tf_op jit(solution)/shard_map/ppermute | solution.py:223
  40.2 7.8 %collective-permute-start.3 = (bf16[128,1024]{1,0:T(8,128)(2,1)}, bf16[128,1024]{1,0:T(8,128)(2,1)S(1)}, u32[]{:S(2)}, u32[]{:S(2)}) collective-permute-start(bf16[128,1024]{1,0:T(8,128)(2,1)} %encode.1.x.ms), channel_id=1, source_target_pairs={{0,6},{1,7},{2,0},{3,1},{4,2},{5,3},{6,4},{7,5},{8,14},{9,15},{10,... | collective-permute-start | bytes 786440 | tf_op jit(solution)/shard_map/ppermute | solution.py:224
  48.1 11.1 %collective-permute-start.7 = (bf16[256,1024]{1,0:T(8,128)(2,1)S(1)}, bf16[256,1024]{1,0:T(8,128)(2,1)S(1)}, u32[]{:S(2)}, u32[]{:S(2)}) collective-permute-start(bf16[256,1024]{1,0:T(8,128)(2,1)S(1)} %pad_maximum_fusion), channel_id=1, source_target_pairs={{0,1},{1,0},{2,3},{3,2},{4,5},{5,4},{6,7},{7,6},{8,9},{9,8},{10,11... | collective-permute-start | bytes 1572872 | tf_op jit(solution)/shard_map/ppermute | solution.py:228
  48.2 7.5 %collective-permute-start.4 = (bf16[64,1024]{1,0:T(8,128)(2,1)S(1)}, bf16[64,1024]{1,0:T(8,128)(2,1)S(1)}, u32[]{:S(2)}, u32[]{:S(2)}) collective-permute-start(bf16[64,1024]{1,0:T(8,128)(2,1)S(1)} %slice.24), channel_id=1, source_target_pairs={{0,2},{1,3},{2,4},{3,5},{4,6},{5,7},{6,0},{7,1},{8,10},{9,11},{10,... | collective-permute-start | bytes 393224 | tf_op jit(solution)/shard_map/ppermute | solution.py:226
  48.3 7.4 %collective-permute-start.5 = (bf16[64,1024]{1,0:T(8,128)(2,1)S(1)}, bf16[64,1024]{1,0:T(8,128)(2,1)S(1)}, u32[]{:S(2)}, u32[]{:S(2)}) collective-permute-start(bf16[64,1024]{1,0:T(8,128)(2,1)S(1)} %slice.25), channel_id=1, source_target_pairs={{0,6},{1,7},{2,0},{3,1},{4,2},{5,3},{6,4},{7,5},{8,14},{9,15},{10,... | collective-permute-start | bytes 393224 | tf_op jit(solution)/shard_map/ppermute | solution.py:227
  51.6 7.5 %collective-permute-start.6 = (bf16[128,1024]{1,0:T(8,128)(2,1)}, bf16[128,1024]{1,0:T(8,128)(2,1)S(1)}, u32[]{:S(2)}, u32[]{:S(2)}) collective-permute-start(bf16[128,1024]{1,0:T(8,128)(2,1)} %encode.1.x.ms), channel_id=1, source_target_pairs={{0,1},{1,0},{2,3},{3,2},{4,5},{5,4},{6,7},{7,6},{8,9},{9,8},{10,11... | collective-permute-start | bytes 786440 | tf_op jit(solution)/shard_map/ppermute | solution.py:225
  55.7 3.4 %collective-permute-start.8 = (bf16[128,1024]{1,0:T(8,128)(2,1)S(1)}, bf16[128,1024]{1,0:T(8,128)(2,1)S(1)}, u32[]{:S(2)}, u32[]{:S(2)}) collective-permute-start(bf16[128,1024]{1,0:T(8,128)(2,1)S(1)} %pad_maximum_fusion.2), channel_id=1, source_target_pairs={{0,1},{1,0},{2,3},{3,2},{4,5},{5,4},{6,7},{7,6},{8,9},{9,8},{10,11... | collective-permute-start | bytes 786440 | tf_op jit(solution)/shard_map/ppermute | solution.py:229
  55.8 14.9 %collective-permute-start.11 = (bf16[128,1024]{1,0:T(8,128)(2,1)S(1)}, bf16[128,1024]{1,0:T(8,128)(2,1)S(1)}, u32[]{:S(2)}, u32[]{:S(2)}) collective-permute-start(bf16[128,1024]{1,0:T(8,128)(2,1)S(1)} %copy-done.8), channel_id=1, source_target_pairs={{0,2},{1,3},{2,4},{3,5},{4,6},{5,7},{6,0},{7,1},{8,10},{9,11},{10,... | collective-permute-start | bytes 786440 | tf_op jit(solution)/shard_map/ppermute | solution.py:223
  57.1 13.7 %collective-permute-start.12 = (bf16[128,1024]{1,0:T(8,128)(2,1)S(1)}, bf16[128,1024]{1,0:T(8,128)(2,1)S(1)}, u32[]{:S(2)}, u32[]{:S(2)}) collective-permute-start(bf16[128,1024]{1,0:T(8,128)(2,1)S(1)} %copy-done.8), channel_id=1, source_target_pairs={{0,6},{1,7},{2,0},{3,1},{4,2},{5,3},{6,4},{7,5},{8,14},{9,15},{10,... | collective-permute-start | bytes 786440 | tf_op jit(solution)/shard_map/ppermute | solution.py:224
  64.6 13.1 %collective-permute-start.10 = (bf16[512,256]{1,0:T(8,128)(2,1)}, bf16[512,256]{1,0:T(8,128)(2,1)S(1)}, u32[]{:S(2)}, u32[]{:S(2)}) collective-permute-start(bf16[512,256]{1,0:T(8,128)(2,1)} %get-tuple-element.10.kva), channel_id=1, source_target_pairs={{8,0},{16,8},{24,16},{32,24},{40,32},{48,40},{56,48},{64,56},{72,6... | collective-permute-start | bytes 786440 | tf_op jit(solution)/shard_map/ppermute | solution.py:350
  68.7 12.1 %collective-permute-start.9 = (bf16[512,256]{1,0:T(8,128)(2,1)}, bf16[512,256]{1,0:T(8,128)(2,1)S(1)}, u32[]{:S(2)}, u32[]{:S(2)}) collective-permute-start(bf16[512,256]{1,0:T(8,128)(2,1)} %get-tuple-element.9.kvb), channel_id=1, source_target_pairs={{0,8},{8,16},{16,24},{24,32},{32,40},{40,48},{48,56},{56,64},{64,7... | collective-permute-start | bytes 786440 | tf_op jit(solution)/shard_map/ppermute | solution.py:349
  70.6 17.6 %copy-start = (bf16[128,1024]{1,0:T(8,128)(2,1)}, bf16[128,1024]{1,0:T(8,128)(2,1)S(1)}, u32[]{:S(2)}) copy-start(bf16[128,1024]{1,0:T(8,128)(2,1)S(1)} %collective-permute-done.11.r1) | copy-start | bytes 786436
  70.7 6.4 %collective-permute-start.13 = (bf16[64,1024]{1,0:T(8,128)(2,1)S(1)}, bf16[64,1024]{1,0:T(8,128)(2,1)S(1)}, u32[]{:S(2)}, u32[]{:S(2)}) collective-permute-start(bf16[64,1024]{1,0:T(8,128)(2,1)S(1)} %slice.26), channel_id=1, source_target_pairs={{0,2},{1,3},{2,4},{3,5},{4,6},{5,7},{6,0},{7,1},{8,10},{9,11},{10,... | collective-permute-start | bytes 393224 | tf_op jit(solution)/shard_map/ppermute | solution.py:226
  70.8 17.4 %copy-start.1 = (bf16[128,1024]{1,0:T(8,128)(2,1)}, bf16[128,1024]{1,0:T(8,128)(2,1)S(1)}, u32[]{:S(2)}) copy-start(bf16[128,1024]{1,0:T(8,128)(2,1)S(1)} %collective-permute-done.12.l1) | copy-start | bytes 786436
  70.8 6.2 %collective-permute-start.14 = (bf16[64,1024]{1,0:T(8,128)(2,1)S(1)}, bf16[64,1024]{1,0:T(8,128)(2,1)S(1)}, u32[]{:S(2)}, u32[]{:S(2)}) collective-permute-start(bf16[64,1024]{1,0:T(8,128)(2,1)S(1)} %slice.27), channel_id=1, source_target_pairs={{0,6},{1,7},{2,0},{3,1},{4,2},{5,3},{6,4},{7,5},{8,14},{9,15},{10,... | collective-permute-start | bytes 393224 | tf_op jit(solution)/shard_map/ppermute | solution.py:227
  74.1 17.6 %collective-permute-start.15 = (bf16[128,1024]{1,0:T(8,128)(2,1)S(1)}, bf16[128,1024]{1,0:T(8,128)(2,1)S(1)}, u32[]{:S(2)}, u32[]{:S(2)}) collective-permute-start(bf16[128,1024]{1,0:T(8,128)(2,1)S(1)} %copy-done.8), channel_id=1, source_target_pairs={{0,1},{1,0},{2,3},{3,2},{4,5},{5,4},{6,7},{7,6},{8,9},{9,8},{10,11... | collective-permute-start | bytes 786440 | tf_op jit(solution)/shard_map/ppermute | solution.py:225
  77.0 11.2 %copy-start.5 = (bf16[64,1024]{1,0:T(8,128)(2,1)}, bf16[64,1024]{1,0:T(8,128)(2,1)S(1)}, u32[]{:S(2)}) copy-start(bf16[64,1024]{1,0:T(8,128)(2,1)S(1)} %collective-permute-done.13.a) | copy-start | bytes 393220
  77.0 14.7 %collective-permute-start.16 = (bf16[256,1024]{1,0:T(8,128)(2,1)S(1)}, bf16[256,1024]{1,0:T(8,128)(2,1)S(1)}, u32[]{:S(2)}, u32[]{:S(2)}) collective-permute-start(bf16[256,1024]{1,0:T(8,128)(2,1)S(1)} %pad_maximum_fusion.1), channel_id=1, source_target_pairs={{0,1},{1,0},{2,3},{3,2},{4,5},{5,4},{6,7},{7,6},{8,9},{9,8},{10,11... | collective-permute-start | bytes 1572872 | tf_op jit(solution)/shard_map/ppermute | solution.py:228
  77.0 11.2 %copy-start.6 = (bf16[64,1024]{1,0:T(8,128)(2,1)}, bf16[64,1024]{1,0:T(8,128)(2,1)S(1)}, u32[]{:S(2)}) copy-start(bf16[64,1024]{1,0:T(8,128)(2,1)S(1)} %collective-permute-done.14.b) | copy-start | bytes 393220
  77.1 14.6 %collective-permute-start.17 = (bf16[128,1024]{1,0:T(8,128)(2,1)S(1)}, bf16[128,1024]{1,0:T(8,128)(2,1)S(1)}, u32[]{:S(2)}, u32[]{:S(2)}) collective-permute-start(bf16[128,1024]{1,0:T(8,128)(2,1)S(1)} %pad_maximum_fusion.3), channel_id=1, source_target_pairs={{0,1},{1,0},{2,3},{3,2},{4,5},{5,4},{6,7},{7,6},{8,9},{9,8},{10,11... | collective-permute-start | bytes 786440 | tf_op jit(solution)/shard_map/ppermute | solution.py:229
  88.2 10.9 %all-to-all-start = ((bf16[8,128,128]{2,1,0:T(8,128)(2,1)}), bf16[8,128,128]{2,1,0:T(8,128)(2,1)S(1)}, u32[]{:S(2)}, u32[]{:S(2)}) async-start(bf16[8,128,128]{2,1,0:T(8,128)(2,1)} %window.1), calls=%async_computation | async-start | bytes 524288 | tf_op jit(solution)/shard_map/all_to_all | solution.py:352
  (15 other events, 60.1 us)
